TPU v7x, 256 devices: a whole 4x4x8 slice. The times are simulated.
256 devices in a mesh: rp: 8 (over x, z_lo), pb: 32 (over z_hi, y, core).
Axes of the slice: x: 4, y: 4, z: 8 (z_hi: 4, z_lo: 2; z = z_hi * 2 + z_lo), core: 2. Of those that a mesh axis runs over, the one named last changes fastest.
Arguments:
- wannier_g: bfloat16 [2, 1024, 32, 1152], P(None, 'rp', 'pb'), may hold values from -0.19921875 to 0.19921875
- rp_coords: int32 [3, 1024], replicated, may hold values from -8 to 8
- q_coords: int32 [3, 512], P(None, ('rp', 'pb')), may hold values from 0 to 15
- k_index: int32 [1], replicated, may hold values from 0 to 7
- k_vectors: bfloat16 [8, 2, 32, 32], replicated, may hold values from -0.75 to 0.75
- kq_vectors: bfloat16 [512, 2, 32, 32], P(('rp', 'pb')), may hold values from -0.75 to 0.75
- modes: bfloat16 [512, 2, 36, 36], P(('rp', 'pb')), may hold values from -0.75 to 0.75
Outputs:
- rotated: float32 [512, 2, 32, 1152], P(('rp', 'pb'))
All inputs are finite; a program needn't handle non-finite values.
Results may differ from a plain program's by a relative error of at most 0.0054.
Values may be sent and summed in bfloat16 or wider, within the bound.
A program may use at most 64 MiB of HBM per device.

v0:
```python
import math
import jax
import jax.numpy as jnp
from jax import lax
from jax.sharding import PartitionSpec as P

NK = 16


def in_blocks(x, dim, length):
    shape = x.shape
    parts = x.reshape(*shape[:dim], length, shape[dim] // length, *shape[dim + 1 :])
    return jnp.moveaxis(parts, dim, 0)


def joined_along(parts, dim):
    shape = list(parts.shape[1:])
    shape[dim] *= parts.shape[0]
    return jnp.moveaxis(parts, 0, dim).reshape(shape)


def one_exchange(x, axis, axes, splits, concats):
    sizes = [lax.axis_size(a) for a in axes]
    parts = in_blocks(x, splits[0], sizes[0])
    parts = jnp.moveaxis(in_blocks(parts, splits[1] + 1, sizes[1]), 0, 1)
    inside = parts.shape[2:]
    parts = parts.reshape(-1, *inside)
    parts = lax.all_to_all(parts, axis, split_axis=0, concat_axis=0, tiled=True)
    parts = joined_along(parts.reshape(*sizes, *inside), concats[0] + 1)
    return joined_along(parts, concats[1])


def phases(q_rows, r_coords):
    turns = jnp.mod(jnp.sum(q_rows[:, :, None] * r_coords[:, None, :], axis=0), NK)
    angle = turns.astype(jnp.float32) * (2.0 * math.pi / NK)
    cosine = jnp.cos(angle).astype(jnp.bfloat16)
    sine = jnp.sin(angle).astype(jnp.bfloat16)
    return (jnp.concatenate([cosine, -sine], axis=1), jnp.concatenate([sine, cosine], axis=1))


def rotate(fourier, mode_vecs, unit, kq_vecs):
    count = fourier.shape[0]
    bands = kq_vecs.shape[2]
    branches = mode_vecs.shape[2]
    field = fourier.reshape(count, 2, bands, bands, branches)
    e_real, e_imag = (mode_vecs[:, 0], mode_vecs[:, 1])
    e_block = jnp.stack([jnp.stack([e_real, e_imag], 2), jnp.stack([-e_imag, e_real], 2)], 1)
    by_mode = jnp.einsum(
        "qcmnv,qcvdu->qdmnu", field, e_block, preferred_element_type=jnp.float32
    ).astype(jnp.bfloat16)
    u_real, u_imag = (unit[0], unit[1])
    u_block = jnp.stack([jnp.stack([u_real, u_imag], 1), jnp.stack([-u_imag, u_real], 1)], 0)
    by_band = jnp.einsum(
        "qcmnu,cndj->qdmju", by_mode, u_block, preferred_element_type=jnp.float32
    ).astype(jnp.bfloat16)
    v_real, v_imag = (kq_vecs[:, 0], kq_vecs[:, 1])
    v_block = jnp.stack([jnp.stack([v_real, -v_imag], 2), jnp.stack([v_imag, v_real], 2)], 1)
    result = jnp.einsum("qcmju,qcmdi->qdiju", by_band, v_block, preferred_element_type=jnp.float32)
    return result.reshape(count, 2, bands, bands * branches)


def local(wannier_g, rp_coords, q_coords, k_index, k_vectors, kq_vectors, modes):
    q_all = lax.all_gather(q_coords, ("rp", "pb"), axis=1, tiled=True)
    total = q_all.shape[1]
    groups = lax.axis_size("rp")
    block = total // groups
    moved = lax.all_to_all(wannier_g, "rp", split_axis=3, concat_axis=1, tiled=True)
    right = moved.reshape(2 * moved.shape[1], -1)
    q_blocks = q_all.reshape(3, groups, block).transpose(1, 0, 2)

    def fourier_block(q_rows):
        left_real, left_imag = phases(q_rows, rp_coords)
        f_real = jnp.dot(left_real, right, preferred_element_type=jnp.float32).astype(jnp.bfloat16)
        f_imag = jnp.dot(left_imag, right, preferred_element_type=jnp.float32).astype(jnp.bfloat16)
        return jnp.stack([f_real, f_imag], 1)

    fourier = lax.map(fourier_block, q_blocks).reshape(total, 2, moved.shape[2], moved.shape[3])
    owned = one_exchange(fourier, ("rp", "pb"), ("rp", "pb"), (0, 0), (3, 2))
    select = (jnp.arange(k_vectors.shape[0]) == k_index[0]).astype(jnp.bfloat16)
    unit = jnp.einsum("k,kcnj->cnj", select, k_vectors, preferred_element_type=jnp.float32).astype(
        jnp.bfloat16
    )
    return rotate(owned, modes, unit, kq_vectors)


def solution(mesh):
    return jax.shard_map(
        local,
        mesh=mesh,
        in_specs=(
            P(None, "rp", "pb", None),
            P(),
            P(None, ("rp", "pb")),
            P(),
            P(),
            P(("rp", "pb"), None, None, None),
            P(("rp", "pb"), None, None, None),
        ),
        out_specs=P(("rp", "pb"), None, None, None),
        check_vma=False,
    )
```

profile of v0, /device:TPU:1, one launch (start us, length us, event | category | flops | bytes accessed | tf_op | source)
XLA Modules:
  0.0 424.2 jit_solution(9630580377085636037)
XLA Ops:
  0.0 3.0 copy.101
  3.0 6.2 %all-to-all-start = ((bf16[2,128,1,1152]{1,0,2,3:T(2,128)(2,1)}), bf16[2,128,1,1152]{1,0,2,3:T(2,128)(2,1)S(1)}, u32[]{:S(2)}, u32[]{:S(2)}) async-start(bf16[2,128,1,1152]{1,0,2,3:T(2,128)(2,1)} %copy.101), calls=%async_computation | async-start | bytes 1179648 | tf_op jit(solution)/shard_map/all_to_all | solution.py:67
  10.3 350.8 %all-gather = s32[256,2,3]{2,1,0:T(2,128)S(1)} all-gather(s32[1,2,3]{2,1,0:T(2,128)S(1)} %bitcast.145), channel_id=1, replica_groups=mesh['rp'=8,'pb'=32] {'rp','pb'}, dimensions={0}, use_global_device_ids=true | all-gather | bytes 6168 | tf_op jit(solution)/shard_map/all_gather | solution.py:63
  362.0 27.2 %while.12 = (s32[]{:T(128)}, bf16[8,64,2,144]{3,2,1,0:T(2,128)(2,1)}, s32[8,3,64]{2,0,1:T(8,128)S(1)}, s32[3,1024]{1,0:T(4,128)S(1)}, bf16[2048,144]{1,0:T(8,128)(2,1)S(1)}, /*index=5*/s32[]{:T(128)}) while((s32[]{:T(128)}, bf16[8,64,2,144]{3,2,1,0:T(2,128)(2,1)}, s32[8,3,64]{2,0,1:T(8,128)S(1)}, s32[3,1024]{1,0:T(4,128)S(1)}, ...), condition=%wide.region_2.3_spmd, body=%wide.region_0.2_spmd.sunk | while | flops 78942208 | bytes 3112789 | solution.py:77
  362.1 0.9 cosine_convert_fusion.2
  363.1 1.0 fusion.51
  364.7 0.7 copy_dynamic-update-slice_fusion.2
  365.5 0.9 cosine_convert_fusion.2
  366.5 1.0 fusion.51
  368.1 0.7 copy_dynamic-update-slice_fusion.2
  368.9 0.9 cosine_convert_fusion.2
  369.9 1.0 fusion.51
  371.5 0.7 copy_dynamic-update-slice_fusion.2
  372.3 0.9 cosine_convert_fusion.2
  373.3 1.0 fusion.51
  374.9 0.7 copy_dynamic-update-slice_fusion.2
  375.7 0.9 cosine_convert_fusion.2
  376.6 1.0 fusion.51
  378.2 0.7 copy_dynamic-update-slice_fusion.2
  379.1 0.9 cosine_convert_fusion.2
  380.0 1.0 fusion.51
  381.6 0.7 copy_dynamic-update-slice_fusion.2
  382.5 0.9 cosine_convert_fusion.2
  383.4 1.0 fusion.51
  385.0 0.7 copy_dynamic-update-slice_fusion.2
  385.9 0.9 cosine_convert_fusion.2
  386.8 1.0 fusion.51
  389.1 5.3 %all-to-all-start.1 = ((bf16[256,2,2,1,144]{4,2,1,3,0:T(2,128)(2,1)}), bf16[256,2,2,1,144]{4,2,1,3,0:T(2,128)(2,1)S(1)}, u32[]{:S(2)}, u32[]{:S(2)}) async-start(bf16[256,2,2,1,144]{4,2,1,3,0:T(2,128)(2,1)} %bitcast.38), calls=%async_computation.1 | async-start | bytes 1048576 | tf_op jit(solution)/shard_map/all_to_all | solution.py:28
  394.9 20.4 %all-to-all-done.1 = bf16[256,2,2,1,144]{4,2,1,3,0:T(2,128)(2,1)S(1)} async-done(((bf16[256,2,2,1,144]{4,2,1,3,0:T(2,128)(2,1)}), bf16[256,2,2,1,144]{4,2,1,3,0:T(2,128)(2,1)S(1)}, u32[]{:S(2)}, u32[]{:S(2)}) %all-to-all-start.1) | async-done | bytes 294944 | tf_op jit(solution)/shard_map/all_to_all | solution.py:28
  416.2 2.8 reshape_reshape.3
  420.5 1.2 copy.114
  421.7 2.4 reshape.53
  (86 shorter events, 10.5 us)
Async XLA Ops:
  0.0 9.9 %copy-start = (bf16[8,2,32,32]{3,2,1,0:T(8,128)(2,1)S(1)}, bf16[8,2,32,32]{3,2,1,0:T(8,128)(2,1)}, u32[]{:S(2)}) copy-start(bf16[8,2,32,32]{3,2,1,0:T(8,128)(2,1)} %param.13) | copy-start | bytes 98308
  0.0 10.2 %copy-start.3 = (bf16[2,2,32,32]{3,2,1,0:T(8,128)(2,1)S(1)}, bf16[2,2,32,32]{3,2,1,0:T(8,128)(2,1)}, u32[]{:S(2)}) copy-start(bf16[2,2,32,32]{3,2,1,0:T(8,128)(2,1)} %param.14) | copy-start | bytes 24580
  0.0 10.3 %copy-start.4 = (s32[3,2]{0,1:T(2,128)S(1)}, s32[3,2]{0,1:T(2,128)}, u32[]{:S(2)}) copy-start(s32[3,2]{0,1:T(2,128)} %param.11) | copy-start | bytes 76
  0.0 361.3 %copy-start.2 = (bf16[2,2,36,36]{3,1,2,0:T(2,128)(2,1)S(1)}, bf16[2,2,36,36]{3,1,2,0:T(2,128)(2,1)}, u32[]{:S(2)}) copy-start(bf16[2,2,36,36]{3,1,2,0:T(2,128)(2,1)} %param.15) | copy-start | bytes 31108
  3.0 358.3 %all-to-all-start = ((bf16[2,128,1,1152]{1,0,2,3:T(2,128)(2,1)}), bf16[2,128,1,1152]{1,0,2,3:T(2,128)(2,1)S(1)}, u32[]{:S(2)}, u32[]{:S(2)}) async-start(bf16[2,128,1,1152]{1,0,2,3:T(2,128)(2,1)} %copy.101), calls=%async_computation | async-start | bytes 1179648 | tf_op jit(solution)/shard_map/all_to_all | solution.py:67
  9.2 352.8 %copy-start.1 = (s32[3,1024]{1,0:T(4,128)S(1)}, s32[3,1024]{1,0:T(4,128)}, u32[]{:S(2)}) copy-start(s32[3,1024]{1,0:T(4,128)} %param.10) | copy-start | bytes 36868
  389.1 26.2 %all-to-all-start.1 = ((bf16[256,2,2,1,144]{4,2,1,3,0:T(2,128)(2,1)}), bf16[256,2,2,1,144]{4,2,1,3,0:T(2,128)(2,1)S(1)}, u32[]{:S(2)}, u32[]{:S(2)}) async-start(bf16[256,2,2,1,144]{4,2,1,3,0:T(2,128)(2,1)} %bitcast.38), calls=%async_computation.1 | async-start | bytes 1048576 | tf_op jit(solution)/shard_map/all_to_all | solution.py:28
where the time goes:
time: 424 us
  blocking collectives  351 us (83%)
  waiting for transfers between devices  20.4 us (5%)
  local copies, waits for them, and re-layouts  17 us (4%)
  other arithmetic  16.8 us (4%)
  starting transfers between devices  11.5 us (3%)
  matrix products  6.36 us (2%)
    all_gather x1, blocking collectives, local(): q_all = lax.all_gather(q_coords, ('rp', 'pb'), axis=1, tiled=True)  351 us
    all_to_all x1, waiting for transfers between devices, one_exchange(): parts = lax.all_to_all(parts, axis, split_axis=0, concat_axis=0, tiled=True)  20.4 us
  transfers between devices with their start and end apart: 2, of which 1 were waited for; matrix products, arithmetic and copies ran while one was open for 0% of the time, Pallas kernels for 0%

commit v1 on v0

--- a/solution.py
+++ b/solution.py
@@ -60,7 +60,7 @@
 
 
 def local(wannier_g, rp_coords, q_coords, k_index, k_vectors, kq_vectors, modes):
-    q_all = lax.all_gather(q_coords, ("rp", "pb"), axis=1, tiled=True)
+    q_all = jnp.concatenate(jax.lax.all_gather(q_coords, ("rp", "pb")), axis=1)
     total = q_all.shape[1]
     groups = lax.axis_size("rp")
     block = total // groups

time: 424 us -> 424 us (level)
  no operation moved by 1% of the time
where the time goes in v1:
time: 424 us
  blocking collectives  351 us (83%)
  waiting for transfers between devices  20.4 us (5%)
  local copies, waits for them, and re-layouts  16.9 us (4%)
  other arithmetic  16.8 us (4%)
  starting transfers between devices  11.5 us (3%)
  matrix products  6.36 us (2%)
    all_gather x1, blocking collectives, local(): q_all = jnp.concatenate(jax.lax.all_gather(q_coords, ('rp', 'pb')), axis=1)  351 us
    all_to_all x1, waiting for transfers between devices, one_exchange(): parts = lax.all_to_all(parts, axis, split_axis=0, concat_axis=0, tiled=True)  20.4 us
  transfers between devices with their start and end apart: 2, of which 1 were waited for; matrix products, arithmetic and copies ran while one was open for 0% of the time, Pallas kernels for 0%

profile of v1, /device:TPU:1, one launch (start us, length us, event | category | flops | bytes accessed | tf_op | source)
XLA Modules:
  0.0 424.0 jit_solution(14274803977324020886)
XLA Ops:
  0.0 3.0 copy.98
  3.0 6.2 %all-to-all-start = ((bf16[2,128,1,1152]{1,0,2,3:T(2,128)(2,1)}), bf16[2,128,1,1152]{1,0,2,3:T(2,128)(2,1)S(1)}, u32[]{:S(2)}, u32[]{:S(2)}) async-start(bf16[2,128,1,1152]{1,0,2,3:T(2,128)(2,1)} %copy.98), calls=%async_computation | async-start | bytes 1179648 | tf_op jit(solution)/shard_map/all_to_all | solution.py:67
  10.3 350.8 %all-gather.1 = s32[256,3,2]{1,2,0:T(2,128)S(1)} all-gather(s32[1,3,2]{1,2,0:T(2,128)S(1)} %bitcast.141), channel_id=2, replica_groups=mesh['rp'=8,'pb'=32] {'rp','pb'}, dimensions={0}, use_global_device_ids=true | all-gather | bytes 6168 | tf_op jit(solution)/shard_map/all_gather | solution.py:63
  361.9 27.1 %while.12 = (s32[]{:T(128)}, bf16[8,64,2,144]{3,2,1,0:T(2,128)(2,1)}, s32[8,3,64]{2,1,0:T(4,128)S(1)}, s32[3,1024]{1,0:T(4,128)S(1)}, bf16[2048,144]{1,0:T(8,128)(2,1)S(1)}, /*index=5*/s32[]{:T(128)}) while((s32[]{:T(128)}, bf16[8,64,2,144]{3,2,1,0:T(2,128)(2,1)}, s32[8,3,64]{2,1,0:T(4,128)S(1)}, s32[3,1024]{1,0:T(4,128)S(1)}, ...), condition=%wide.region_2.3_spmd, body=%wide.region_0.2_spmd.sunk | while | flops 78942208 | bytes 3111253 | solution.py:77
  362.1 0.9 cosine_convert_fusion.2
  363.0 1.0 fusion.51
  364.6 0.7 copy_dynamic-update-slice_fusion.2
  365.4 0.9 cosine_convert_fusion.2
  366.4 1.0 fusion.51
  368.0 0.7 copy_dynamic-update-slice_fusion.2
  368.8 0.9 cosine_convert_fusion.2
  369.8 1.0 fusion.51
  371.4 0.7 copy_dynamic-update-slice_fusion.2
  372.2 0.9 cosine_convert_fusion.2
  373.2 1.0 fusion.51
  374.8 0.7 copy_dynamic-update-slice_fusion.2
  375.6 0.9 cosine_convert_fusion.2
  376.5 1.0 fusion.51
  378.1 0.7 copy_dynamic-update-slice_fusion.2
  379.0 0.9 cosine_convert_fusion.2
  379.9 1.0 fusion.51
  381.5 0.7 copy_dynamic-update-slice_fusion.2
  382.4 0.9 cosine_convert_fusion.2
  383.3 1.0 fusion.51
  384.9 0.7 copy_dynamic-update-slice_fusion.2
  385.7 0.9 cosine_convert_fusion.2
  386.7 1.0 fusion.51
  389.0 5.3 %all-to-all-start.1 = ((bf16[256,2,2,1,144]{4,2,1,3,0:T(2,128)(2,1)}), bf16[256,2,2,1,144]{4,2,1,3,0:T(2,128)(2,1)S(1)}, u32[]{:S(2)}, u32[]{:S(2)}) async-start(bf16[256,2,2,1,144]{4,2,1,3,0:T(2,128)(2,1)} %bitcast.37), calls=%async_computation.1 | async-start | bytes 1048576 | tf_op jit(solution)/shard_map/all_to_all | solution.py:28
  394.8 20.4 %all-to-all-done.1 = bf16[256,2,2,1,144]{4,2,1,3,0:T(2,128)(2,1)S(1)} async-done(((bf16[256,2,2,1,144]{4,2,1,3,0:T(2,128)(2,1)}), bf16[256,2,2,1,144]{4,2,1,3,0:T(2,128)(2,1)S(1)}, u32[]{:S(2)}, u32[]{:S(2)}) %all-to-all-start.1) | async-done | bytes 294944 | tf_op jit(solution)/shard_map/all_to_all | solution.py:28
  416.1 2.8 reshape_reshape.7
  420.4 1.2 copy.110
  421.6 2.4 reshape.53
  (77 shorter events, 10.4 us)
Async XLA Ops:
  0.0 9.9 %copy-start = (bf16[8,2,32,32]{3,2,1,0:T(8,128)(2,1)S(1)}, bf16[8,2,32,32]{3,2,1,0:T(8,128)(2,1)}, u32[]{:S(2)}) copy-start(bf16[8,2,32,32]{3,2,1,0:T(8,128)(2,1)} %param.13) | copy-start | bytes 98308
  0.0 10.2 %copy-start.3 = (bf16[2,2,32,32]{3,2,1,0:T(8,128)(2,1)S(1)}, bf16[2,2,32,32]{3,2,1,0:T(8,128)(2,1)}, u32[]{:S(2)}) copy-start(bf16[2,2,32,32]{3,2,1,0:T(8,128)(2,1)} %param.14) | copy-start | bytes 24580
  0.0 10.3 %copy-start.4 = (s32[3,2]{0,1:T(2,128)S(1)}, s32[3,2]{0,1:T(2,128)}, u32[]{:S(2)}) copy-start(s32[3,2]{0,1:T(2,128)} %param.11) | copy-start | bytes 76
  0.0 361.2 %copy-start.2 = (bf16[2,2,36,36]{3,1,2,0:T(2,128)(2,1)S(1)}, bf16[2,2,36,36]{3,1,2,0:T(2,128)(2,1)}, u32[]{:S(2)}) copy-start(bf16[2,2,36,36]{3,1,2,0:T(2,128)(2,1)} %param.15) | copy-start | bytes 31108
  3.0 358.3 %all-to-all-start = ((bf16[2,128,1,1152]{1,0,2,3:T(2,128)(2,1)}), bf16[2,128,1,1152]{1,0,2,3:T(2,128)(2,1)S(1)}, u32[]{:S(2)}, u32[]{:S(2)}) async-start(bf16[2,128,1,1152]{1,0,2,3:T(2,128)(2,1)} %copy.98), calls=%async_computation | async-start | bytes 1179648 | tf_op jit(solution)/shard_map/all_to_all | solution.py:67
  9.2 352.7 %copy-start.1 = (s32[3,1024]{1,0:T(4,128)S(1)}, s32[3,1024]{1,0:T(4,128)}, u32[]{:S(2)}) copy-start(s32[3,1024]{1,0:T(4,128)} %param.10) | copy-start | bytes 36868
  389.0 26.2 %all-to-all-start.1 = ((bf16[256,2,2,1,144]{4,2,1,3,0:T(2,128)(2,1)}), bf16[256,2,2,1,144]{4,2,1,3,0:T(2,128)(2,1)S(1)}, u32[]{:S(2)}, u32[]{:S(2)}) async-start(bf16[256,2,2,1,144]{4,2,1,3,0:T(2,128)(2,1)} %bitcast.37), calls=%async_computation.1 | async-start | bytes 1048576 | tf_op jit(solution)/shard_map/all_to_all | solution.py:28
